TPU v7x, 256 devices: a whole 4x4x8 slice. The times are simulated.
256 devices in a mesh: group: 4 (over x), dp: 16 (over z_lo, y, core), mp: 4 (over z_hi).
Axes of the slice: x: 4, y: 4, z: 8 (z_hi: 4, z_lo: 2; z = z_hi * 2 + z_lo), core: 2. Of those that a mesh axis runs over, the one named last changes fastest.
Arguments:
- block_input: bfloat16 [768, 8192], P(None, 'dp'), may hold values from -6 to 6
- parent_gate_up: bfloat16 [2, 8192, 14336], P(None, 'dp', ('group', 'mp')), may hold values from -0.0625 to 0.0625
- parent_down: bfloat16 [14336, 8192], P(('group', 'mp'), 'dp'), may hold values from -0.046875 to 0.046875
- variant_gate_up: bfloat16 [4, 2, 8192, 3584], P('group', None, 'dp', 'mp'), may hold values from -0.0625 to 0.0625
- variant_down: bfloat16 [4, 3584, 8192], P('group', 'mp', 'dp'), may hold values from -0.09375 to 0.09375
- widths: int32 [4], P('group'), may hold values from 896 to 3584, as said below
Outputs:
- grad_gate_up: float32 [4, 2, 8192, 3584], P('group', None, 'dp', 'mp')
- grad_down: float32 [4, 3584, 8192], P('group', 'mp', 'dp')
Inputs may be any that keep to these rules, and one draw needn't show every extreme that they name: Variant v uses its hidden units 0 to widths[v] - 1; one variant uses all 3584 of them and another exactly a quarter of 3584.
All inputs are finite; a program needn't handle non-finite values.
Results may differ from a plain program's by a relative error of at most 0.008.
Values may be sent and summed in bfloat16 or wider, within the bound.
No kernel may reach another device: no remote copies, remote signals or barrier semaphores. Data moves between devices by JAX's collectives and lax.ppermute only.
A program may use at most 64 MiB of HBM per device.

v0:
```python
import math
import jax
import jax.numpy as jnp
from jax import lax
from jax.sharding import PartitionSpec as P


def gated_values(pre_act, unit_mask):
    gate_value = pre_act[:, 0].astype(jnp.float32)
    up_value = pre_act[:, 1].astype(jnp.float32)
    sigmoid_gate = jax.nn.sigmoid(gate_value)
    return (gate_value * sigmoid_gate * up_value * unit_mask).astype(jnp.bfloat16)


def pre_gradient(pre_act, unit_mask, hidden_grad):
    gate_value = pre_act[:, 0].astype(jnp.float32)
    up_value = pre_act[:, 1].astype(jnp.float32)
    sigmoid_gate = jax.nn.sigmoid(gate_value)
    masked_grad = hidden_grad * unit_mask
    grad_gate = masked_grad * up_value * sigmoid_gate * (1.0 + gate_value * (1.0 - sigmoid_gate))
    grad_up = masked_grad * gate_value * sigmoid_gate
    return jnp.stack([grad_gate, grad_up], axis=1).astype(jnp.bfloat16)


def body(block_input, parent_gate_up, parent_down, variant_gate_up, variant_down, widths):
    local_gate_up = variant_gate_up[0]
    local_down = variant_down[0]
    local_units = local_down.shape[0]
    all_tokens = block_input.shape[0]
    first_unit = lax.axis_index("mp") * local_units
    unit_index = first_unit + jnp.arange(local_units, dtype=jnp.int32)
    unit_mask = (unit_index < widths[0]).astype(jnp.float32)
    parent_term = jnp.einsum(
        "td,kdf->tkf", block_input, parent_gate_up, preferred_element_type=jnp.float32
    )
    variant_term = jnp.einsum(
        "td,kdf->tkf", block_input, local_gate_up, preferred_element_type=jnp.float32
    )
    parent_rows, variant_rows = (
        lax.psum_scatter(parent_term, "dp", scatter_dimension=0, tiled=True),
        lax.psum_scatter(variant_term, "dp", scatter_dimension=0, tiled=True),
    )
    parent_pre = parent_rows.astype(jnp.bfloat16)
    variant_pre = variant_rows.astype(jnp.bfloat16)
    parent_hidden = gated_values(parent_pre, 1.0)
    parent_all, variant_all = (
        lax.all_gather(parent_hidden, "dp", axis=0, tiled=True),
        lax.all_gather(variant_pre, "dp", axis=0, tiled=True),
    )
    variant_hidden = gated_values(variant_all, unit_mask)
    teacher_part = jnp.dot(parent_all, parent_down, preferred_element_type=jnp.float32)
    student_part = jnp.dot(variant_hidden, local_down, preferred_element_type=jnp.float32)
    teacher = lax.psum(teacher_part, ("group", "mp"))
    student = lax.psum(student_part, "mp")
    loss_scale = 1.0 / math.sqrt(all_tokens)
    output_grad = ((student - teacher) * loss_scale).astype(jnp.bfloat16)
    grad_down = lax.dot_general(
        variant_hidden, output_grad, (((0,), (0,)), ((), ())), preferred_element_type=jnp.float32
    )
    hidden_part = lax.dot_general(
        output_grad, local_down, (((1,), (1,)), ((), ())), preferred_element_type=jnp.float32
    )
    hidden_full = lax.psum(hidden_part, "dp")
    grad_pre = pre_gradient(variant_all, unit_mask, hidden_full)
    grad_gate_up = jnp.einsum(
        "td,tkf->kdf", block_input, grad_pre, preferred_element_type=jnp.float32
    )
    return (grad_gate_up[None], grad_down[None])


def solution(mesh):
    in_specs = (
        P(None, "dp"),
        P(None, "dp", ("group", "mp")),
        P(("group", "mp"), "dp"),
        P("group", None, "dp", "mp"),
        P("group", "mp", "dp"),
        P("group"),
    )
    out_specs = (P("group", None, "dp", "mp"), P("group", "mp", "dp"))
    return jax.shard_map(body, mesh=mesh, in_specs=in_specs, out_specs=out_specs, check_vma=False)
```

profile of v0, /device:TPU:1, one launch (start us, length us, event | category | flops | bytes accessed | tf_op | source)
XLA Modules:
  0.0 652.1 jit_solution(2625803845936884595)
XLA Ops:
  7.2 0.0 copy-start
  7.2 0.0 reduce-scatter.5.cloned.1.call-start
  7.2 1.4 copy-done
  8.7 5.2 fusion.45
  13.9 0.0 copy-start.1
  13.9 0.0 reduce-scatter.5.cloned.1.call-update
  13.9 0.0 reduce-scatter.3.cloned.1.call-start
  13.9 1.1 copy-done.1
  15.0 5.5 fusion.29
  20.5 0.0 reduce-scatter.3.cloned.1.call-update
  20.5 0.0 all-gather.5.cloned.1.call-start
  20.6 66.0 %reduce-scatter.5.cloned.1.call-done = f32[48,2,896]{2,0,1:T(8,128)} async-done(((f32[768,2,896]{2,0,1:T(8,128)}), f32[48,2,896]{2,0,1:T(8,128)}) %reduce-scatter.5.cloned.1.call-update) | async-done | bytes 344080 | tf_op jit(solution)/shard_map/reduce_scatter | solution.py:40
  86.6 1.0 convert_element_type.66
  87.6 0.7 fusion.52
  88.3 0.0 all-gather.5.cloned.1.call-update
  88.3 0.0 all-gather.3.cloned.1.call-start
  88.4 71.3 %reduce-scatter.3.cloned.1.call-done = f32[48,2,896]{2,0,1:T(8,128)} async-done(((f32[768,2,896]{2,0,1:T(8,128)}), f32[48,2,896]{2,0,1:T(8,128)}) %reduce-scatter.3.cloned.1.call-update) | async-done | bytes 344080 | tf_op jit(solution)/shard_map/reduce_scatter | solution.py:41
  159.7 1.7 convert_element_type.60
  161.3 0.0 all-gather.3.cloned.1.call-update
  161.3 0.0 copy-start.2
  161.4 0.0 all-reduce.6.cloned.1.call-start
  161.4 38.0 %all-gather.5.cloned.1.call-done = bf16[768,896]{1,0:T(8,128)(2,1)} async-done(((bf16[48,896]{1,0:T(8,128)(2,1)}), bf16[768,896]{1,0:T(8,128)(2,1)}) %all-gather.5.cloned.1.call-update) | async-done | bytes 1376272 | tf_op jit(solution)/shard_map/all_gather | solution.py:47
  199.4 3.7 fusion.57
  203.1 0.0 all-reduce.6.cloned.1.call-update
  203.1 0.0 all-reduce.4.cloned.1.call-start
  203.8 35.3 %all-gather.3.cloned.1.call-done = bf16[768,2,896]{2,0,1:T(8,128)(2,1)} async-done(((bf16[48,2,896]{2,0,1:T(8,128)(2,1)}), bf16[768,2,896]{2,0,1:T(8,128)(2,1)}) %all-gather.3.cloned.1.call-update) | async-done | bytes 2752528 | tf_op jit(solution)/shard_map/all_gather | solution.py:48
  239.1 0.0 copy-done.2
  239.1 4.0 fusion.31
  243.2 0.0 all-reduce.4.cloned.1.call-update
  243.2 0.0 all-reduce.8.cloned.1.call-start
  243.2 163.2 %all-reduce.6.cloned.1.call-done = f32[768,512]{1,0:T(8,128)} async-done(((f32[768,512]{1,0:T(8,128)}), f32[768,512]{1,0:T(8,128)}) %all-reduce.6.cloned.1.call-update) | async-done | bytes 1572880 | tf_op jit(solution)/shard_map/psum | solution.py:53
  406.4 93.0 %all-reduce.4.cloned.1.call-done = f32[768,512]{1,0:T(8,128)} async-done(((f32[768,512]{1,0:T(8,128)}), f32[768,512]{1,0:T(8,128)}) %all-reduce.4.cloned.1.call-update) | async-done | bytes 1572880 | tf_op jit(solution)/shard_map/psum | solution.py:54
  499.4 2.3 multiply_convert_fusion
  501.7 3.7 fusion.39
  505.4 0.0 all-reduce.8.cloned.1.call-update
  505.5 4.1 convolution_bitcast_fusion
  509.6 123.6 %all-reduce.8.cloned.1.call-done = f32[768,896]{1,0:T(8,128)} async-done(((f32[768,896]{1,0:T(8,128)}), f32[768,896]{1,0:T(8,128)}) %all-reduce.8.cloned.1.call-update) | async-done | bytes 2752528 | tf_op jit(solution)/shard_map/psum | solution.py:63
  633.2 4.0 fusion.36
  637.2 3.5 fusion.26
  640.7 4.6 copy.9
  (1 shorter events, 0.0 us)
Async XLA Ops:
  7.2 1.5 copy-start
  7.2 79.4 %reduce-scatter.5.cloned.1.call-start = ((), (), s32[]{:S(2)}) async-start(), calls=%async_computation.5 | async-start | bytes 5849088 | tf_op jit(solution)/shard_map/reduce_scatter | solution.py:40
  13.9 1.1 copy-start.1
  13.9 145.8 %reduce-scatter.3.cloned.1.call-start = ((), (), s32[]{:S(2)}) async-start(), calls=%async_computation.2 | async-start | bytes 5849088 | tf_op jit(solution)/shard_map/reduce_scatter | solution.py:41
  20.5 178.9 %all-gather.5.cloned.1.call-start = ((), (), s32[]{:S(2)}) async-start(), calls=%async_computation.6 | async-start | bytes 1462272 | tf_op jit(solution)/shard_map/all_gather | solution.py:47
  88.3 150.8 %all-gather.3.cloned.1.call-start = ((), (), s32[]{:S(2)}) async-start(), calls=%async_computation.3 | async-start | bytes 2924544 | tf_op jit(solution)/shard_map/all_gather | solution.py:48
  161.3 77.8 %copy-start.2 = (bf16[1,896,512]{2,1,0:T(8,128)(2,1)S(1)}, bf16[1,896,512]{2,1,0:T(8,128)(2,1)}, u32[]{:S(2)}) copy-start(bf16[1,896,512]{2,1,0:T(8,128)(2,1)} %param.10) | copy-start | bytes 2752516
  161.4 245.1 %all-reduce.6.cloned.1.call-start = ((), (), s32[]{:S(2)}) async-start(), calls=%async_computation.7 | async-start | bytes 3145728 | tf_op jit(solution)/shard_map/psum | solution.py:53
  203.1 296.3 %all-reduce.4.cloned.1.call-start = ((), (), s32[]{:S(2)}) async-start(), calls=%async_computation.4 | async-start | bytes 3145728 | tf_op jit(solution)/shard_map/psum | solution.py:54
  243.2 390.0 %all-reduce.8.cloned.1.call-start = ((), (), s32[]{:S(2)}) async-start(), calls=%async_computation.8 | async-start | bytes 5505024 | tf_op jit(solution)/shard_map/psum | solution.py:63
Sparse Core Ops, SparseCore 0:
  14.0 72.5 reduce-scatter.4
  89.1 70.4 reduce-scatter.2
  162.1 37.2 all-gather.4
  201.6 37.4 all-gather.2
  242.2 164.1 all-reduce.5
  409.5 89.8 all-reduce.3
  505.6 127.5 all-reduce.7
where the time goes:
time: 653 us; the launch traced here: 652 us
  waiting for transfers between devices  590 us (90%)
  matrix products  29.8 us (5%)
  between operations  14.8 us (2%)
  other arithmetic  9.67 us (1%)
  local copies, waits for them, and re-layouts  7.1 us (1%)
    psum x1, waiting for transfers between devices, body(): teacher = lax.psum(teacher_part, ('group', 'mp'))  163 us
    psum x1, waiting for transfers between devices, body(): hidden_full = lax.psum(hidden_part, 'dp')  124 us
    psum x1, waiting for transfers between devices, body(): student = lax.psum(student_part, 'mp')  93 us
    reduce_scatter x1, waiting for transfers between devices, body(): lax.psum_scatter(variant_term, 'dp', scatter_dimension=0, tiled=True)  71.3 us
    reduce_scatter x1, waiting for transfers between devices, body(): lax.psum_scatter(parent_term, 'dp', scatter_dimension=0, tiled=True)  66 us
    all_gather x1, waiting for transfers between devices, body(): lax.all_gather(parent_hidden, 'dp', axis=0, tiled=True)  38 us
    all_gather x1, waiting for transfers between devices, body(): lax.all_gather(variant_pre, 'dp', axis=0, tiled=True)  35.3 us
  transfers between devices with their start and end apart: 7, of which 7 were waited for; matrix products, arithmetic and copies ran while one was open for 3% of the time, Pallas kernels for 0%

commit v1 on v0

--- a/solution.py
+++ b/solution.py
@@ -51,7 +51,7 @@
     teacher_part = jnp.dot(parent_all, parent_down, preferred_element_type=jnp.float32)
     student_part = jnp.dot(variant_hidden, local_down, preferred_element_type=jnp.float32)
     teacher = lax.psum(teacher_part, ("group", "mp"))
-    student = lax.psum(student_part, "mp")
+    student = jnp.sum(lax.all_gather(student_part, "mp"), axis=0)
     loss_scale = 1.0 / math.sqrt(all_tokens)
     output_grad = ((student - teacher) * loss_scale).astype(jnp.bfloat16)
     grad_down = lax.dot_general(

time: 653 us -> 690 us (1.057)
  waiting for transfers between devices: 590 us -> 623 us
    all_gather x0 -> x1, waiting for transfers between devices: none -> 117 us  [body(): student = jnp.sum(lax.all_gather(student_part, 'mp'), axis=0)]
    psum x1 -> x0, waiting for transfers between devices: 93 us -> none  [body(): student = lax.psum(student_part, 'mp')]
    psum x1, waiting for transfers between devices: 124 us -> 131 us  [body(): hidden_full = lax.psum(hidden_part, 'dp')]
  transfers between devices with their start and end apart: 7 -> 7, of which waited for: 7 -> 7; matrix products, arithmetic and copies ran while one was open for 3% -> 4% of each run, Pallas kernels for 0% -> 0%
where the time goes in v1:
time: 690 us; the launch traced here: 689 us
  waiting for transfers between devices  623 us (90%)
  matrix products  28.5 us (4%)
  between operations  14.8 us (2%)
  other arithmetic  13 us (2%)
  local copies, waits for them, and re-layouts  9.08 us (1%)
    psum x1, waiting for transfers between devices, body(): teacher = lax.psum(teacher_part, ('group', 'mp'))  164 us
    psum x1, waiting for transfers between devices, body(): hidden_full = lax.psum(hidden_part, 'dp')  131 us
    all_gather x1, waiting for transfers between devices, body(): student = jnp.sum(lax.all_gather(student_part, 'mp'), axis=0)  117 us
    reduce_scatter x1, waiting for transfers between devices, body(): lax.psum_scatter(parent_term, 'dp', scatter_dimension=0, tiled=True)  71.3 us
    reduce_scatter x1, waiting for transfers between devices, body(): lax.psum_scatter(variant_term, 'dp', scatter_dimension=0, tiled=True)  66 us
    all_gather x1, waiting for transfers between devices, body(): lax.all_gather(variant_pre, 'dp', axis=0, tiled=True)  39.5 us
    all_gather x1, waiting for transfers between devices, body(): lax.all_gather(parent_hidden, 'dp', axis=0, tiled=True)  33.6 us
  transfers between devices with their start and end apart: 7, of which 7 were waited for; matrix products, arithmetic and copies ran while one was open for 4% of the time, Pallas kernels for 0%

profile of v1, /device:TPU:1, one launch (start us, length us, event | category | flops | bytes accessed | tf_op | source)
XLA Modules:
  0.0 689.2 jit_solution(12115107575456486976)
XLA Ops:
  7.2 0.0 copy-start
  7.2 0.0 reduce-scatter.3.cloned.1.call-start
  7.2 1.4 copy-done
  8.7 5.2 fusion.29
  13.8 0.0 copy-start.3
  13.8 0.0 reduce-scatter.3.cloned.1.call-update
  13.9 0.0 reduce-scatter.5.cloned.1.call-start
  13.9 1.1 copy-done.3
  15.0 5.5 fusion.45
  20.5 0.0 copy-start.5
  20.5 0.0 reduce-scatter.5.cloned.1.call-update
  20.5 0.0 all-gather.5.cloned.1.call-start
  20.5 66.0 %reduce-scatter.3.cloned.1.call-done = f32[48,2,896]{2,0,1:T(8,128)} async-done(((f32[768,2,896]{2,0,1:T(8,128)}), f32[48,2,896]{2,0,1:T(8,128)}) %reduce-scatter.3.cloned.1.call-update) | async-done | bytes 344080 | tf_op jit(solution)/shard_map/reduce_scatter | solution.py:41
  86.6 1.7 convert_element_type.60
  88.2 0.0 all-gather.5.cloned.1.call-update
  88.3 0.0 all-gather.7.cloned.1.call-start
  88.3 71.3 %reduce-scatter.5.cloned.1.call-done = f32[48,2,896]{2,0,1:T(8,128)} async-done(((f32[768,2,896]{2,0,1:T(8,128)}), f32[48,2,896]{2,0,1:T(8,128)}) %reduce-scatter.5.cloned.1.call-update) | async-done | bytes 344080 | tf_op jit(solution)/shard_map/reduce_scatter | solution.py:40
  159.6 1.0 convert_element_type.66
  160.6 0.7 fusion.52
  161.3 0.0 all-gather.7.cloned.1.call-update
  161.4 0.0 all-gather.9.cloned.1.call-start
  162.1 39.5 %all-gather.5.cloned.1.call-done = bf16[768,2,896]{2,0,1:T(8,128)(2,1)} async-done(((bf16[48,2,896]{2,0,1:T(8,128)(2,1)}), bf16[768,2,896]{2,0,1:T(8,128)(2,1)}) %all-gather.5.cloned.1.call-update) | async-done | bytes 2752528 | tf_op jit(solution)/shard_map/all_gather | solution.py:48
  201.6 0.0 copy-done.5
  201.6 4.0 fusion.31
  205.6 0.0 all-gather.9.cloned.1.call-update
  205.6 0.0 all-reduce.3.cloned.1.call-start
  205.7 33.6 %all-gather.7.cloned.1.call-done = bf16[768,896]{1,0:T(8,128)(2,1)} async-done(((bf16[48,896]{1,0:T(8,128)(2,1)}), bf16[768,896]{1,0:T(8,128)(2,1)}) %all-gather.7.cloned.1.call-update) | async-done | bytes 1376272 | tf_op jit(solution)/shard_map/all_gather | solution.py:47
  239.3 3.7 fusion.57
  243.0 0.0 all-reduce.3.cloned.1.call-update
  243.0 0.0 all-reduce.5.cloned.1.call-start
  243.1 117.2 %all-gather.9.cloned.1.call-done = f32[3072,512]{1,0:T(8,128)} async-done(((f32[768,512]{1,0:T(8,128)}), f32[3072,512]{1,0:T(8,128)}) %all-gather.9.cloned.1.call-update) | async-done | bytes 6291472 | tf_op jit(solution)/shard_map/all_gather | solution.py:54
  360.2 3.7 reduce_sum.9
  363.9 164.3 %all-reduce.3.cloned.1.call-done = f32[768,512]{1,0:T(8,128)} async-done(((f32[768,512]{1,0:T(8,128)}), f32[768,512]{1,0:T(8,128)}) %all-reduce.3.cloned.1.call-update) | async-done | bytes 1572880 | tf_op jit(solution)/shard_map/psum | solution.py:53
  528.2 0.0 copy-start.6
  528.2 1.9 multiply_convert_fusion
  530.1 0.0 copy-start.1
  530.1 0.9 copy-done.1
  531.0 0.0 copy-done.6
  531.0 2.5 fusion.39
  533.5 0.0 copy-start.2
  533.5 0.0 all-reduce.5.cloned.1.call-update
  533.6 1.1 copy-done.2
  534.7 4.1 convolution_bitcast_fusion
  538.8 131.5 %all-reduce.5.cloned.1.call-done = f32[768,896]{1,0:T(8,128)} async-done(((f32[768,896]{1,0:T(8,128)}), f32[768,896]{1,0:T(8,128)}) %all-reduce.5.cloned.1.call-update) | async-done | bytes 2752528 | tf_op jit(solution)/shard_map/psum | solution.py:63
  670.3 4.0 fusion.36
  674.3 0.0 copy-done.4
  674.3 3.5 fusion.26
  677.7 4.6 copy.9
  (2 shorter events, 0.0 us)
Async XLA Ops:
  7.2 1.5 copy-start
  7.2 79.4 %reduce-scatter.3.cloned.1.call-start = ((), (), s32[]{:S(2)}) async-start(), calls=%async_computation.2 | async-start | bytes 5849088 | tf_op jit(solution)/shard_map/reduce_scatter | solution.py:41
  13.8 1.1 copy-start.3
  13.9 145.8 %reduce-scatter.5.cloned.1.call-start = ((), (), s32[]{:S(2)}) async-start(), calls=%async_computation.4 | async-start | bytes 5849088 | tf_op jit(solution)/shard_map/reduce_scatter | solution.py:40
  20.5 181.1 %copy-start.5 = (bf16[1,896,512]{2,1,0:T(8,128)(2,1)S(1)}, bf16[1,896,512]{2,1,0:T(8,128)(2,1)}, u32[]{:S(2)}) copy-start(bf16[1,896,512]{2,1,0:T(8,128)(2,1)} %param.10) | copy-start | bytes 2752516
  20.5 181.1 %all-gather.5.cloned.1.call-start = ((), (), s32[]{:S(2)}) async-start(), calls=%async_computation.3 | async-start | bytes 2924544 | tf_op jit(solution)/shard_map/all_gather | solution.py:48
  88.3 151.0 %all-gather.7.cloned.1.call-start = ((), (), s32[]{:S(2)}) async-start(), calls=%async_computation.5 | async-start | bytes 1462272 | tf_op jit(solution)/shard_map/all_gather | solution.py:47
  161.4 198.9 %all-gather.9.cloned.1.call-start = ((), (), s32[]{:S(2)}) async-start(), calls=%async_computation.8 | async-start | bytes 7864320 | tf_op jit(solution)/shard_map/all_gather | solution.py:54
  205.6 322.6 %all-reduce.3.cloned.1.call-start = ((), (), s32[]{:S(2)}) async-start(), calls=%async_computation.6 | async-start | bytes 3145728 | tf_op jit(solution)/shard_map/psum | solution.py:53
  243.0 427.2 %all-reduce.5.cloned.1.call-start = ((), (), s32[]{:S(2)}) async-start(), calls=%async_computation.7 | async-start | bytes 5505024 | tf_op jit(solution)/shard_map/psum | solution.py:63
  528.2 2.8 copy-start.6
  530.1 0.9 copy-start.1
  533.5 1.1 copy-start.2
  538.8 135.5 %copy-start.4 = (bf16[768,512]{1,0:T(8,128)(2,1)S(1)}, bf16[768,512]{1,0:T(8,128)(2,1)}, u32[]{:S(2)}) copy-start(bf16[768,512]{1,0:T(8,128)(2,1)} %param.6) | copy-start | bytes 2359300
Sparse Core Ops, SparseCore 0:
  14.0 72.5 reduce-scatter.2
  89.1 70.4 reduce-scatter.4
  162.0 39.5 all-gather.4
  203.9 35.3 all-gather.6
  241.5 118.6 all-gather.8
  363.3 164.8 all-reduce.2
  533.7 136.5 all-reduce.4
